TPU v7x, 32 devices: a whole 2x2x4 slice. The times are simulated.
32 devices in a mesh: blk: 16 (over z, y, core), head: 2 (over x).
Axes of the slice: x: 2, y: 2, z: 4, core: 2. Of those that a mesh axis runs over, the one named last changes fastest.
Arguments:
- query: bfloat16 [4096, 4096], P(('blk', 'head')), may hold values from -6 to 6
- key: bfloat16 [4096, 1024], P(('blk', 'head')), may hold values from -6 to 6
- value: bfloat16 [4096, 1024], P(('blk', 'head')), may hold values from -6 to 6
- grad_out: bfloat16 [4096, 4096], P(('blk', 'head')), may hold values from -6 to 6
- doc_lengths: int32 [32], replicated, may hold values from 1 to 256, 4096 in all
Outputs:
- attended: bfloat16 [4096, 4096], P(('blk', 'head'))
- grad_query: bfloat16 [4096, 4096], P(('blk', 'head'))
- grad_key: bfloat16 [4096, 1024], P(('blk', 'head'))
- grad_value: bfloat16 [4096, 1024], P(('blk', 'head'))
Inputs may be any that keep to these rules, and one draw needn't show every extreme that they name: `doc_lengths`: every document has at most 256 tokens, one has exactly 256, and the lengths sum to 4096.
All inputs are finite; a program needn't handle non-finite values.
Results may differ from a plain program's by a relative error of at most 0.0088.
Values may be sent and summed in bfloat16 or wider, within the bound.
A program may use at most 128 MiB of HBM per device.

v0:
```python
import jax
import jax.numpy as jnp
from jax import lax
from jax.sharding import PartitionSpec as P

HEAD_DIM = 128


def passed_along(value, axis, steps):
    count = lax.axis_size(axis)
    initial, last = (max(0, -steps), min(count, count - steps))
    return lax.ppermute(value, axis, [(source, source + steps) for source in range(initial, last)])


def segment_ids(positions, doc_starts):
    return jnp.sum((doc_starts[None, :] <= positions[:, None]).astype(jnp.int32), axis=1) - 1


def per_device(query, key, value, grad_out, doc_lengths):
    scaling = HEAD_DIM ** (-0.5)
    query_heads, key_heads, value_heads = (
        lax.all_to_all(query, "head", split_axis=1, concat_axis=0, tiled=True),
        lax.all_to_all(key, "head", split_axis=1, concat_axis=0, tiled=True),
        lax.all_to_all(value, "head", split_axis=1, concat_axis=0, tiled=True),
    )
    block_rows = query_heads.shape[0]
    pair_width = key_heads.shape[1]
    kv_local = pair_width // HEAD_DIM
    groups = query_heads.shape[1] // pair_width
    width_local = query_heads.shape[1]
    tile_rows = min(512, block_rows)
    tile_count = block_rows // tile_rows
    span_rows = block_rows + tile_rows
    block_index = lax.axis_index("blk")
    doc_ends = jnp.cumsum(doc_lengths)
    doc_starts = doc_ends - doc_lengths
    offsets = jnp.arange(tile_rows, dtype=jnp.int32)
    reaches = jnp.arange(span_rows, dtype=jnp.int32)
    paired = jnp.concatenate([key_heads, value_heads], axis=1)
    earlier = passed_along(paired, "blk", 1)
    window = jnp.concatenate([earlier, paired], axis=0)

    def tile_scores(tile_number):
        first_row = tile_number * tile_rows
        query_rows = lax.dynamic_slice_in_dim(query_heads, first_row, tile_rows, 0).reshape(
            tile_rows, kv_local, groups, HEAD_DIM
        )
        span_pairs = lax.dynamic_slice_in_dim(window, first_row, span_rows, 0)
        key_rows = span_pairs[:, :pair_width].reshape(span_rows, kv_local, HEAD_DIM)
        value_rows = span_pairs[:, pair_width:].reshape(span_rows, kv_local, HEAD_DIM)
        query_pos = block_index * block_rows + first_row + offsets
        key_pos = block_index * block_rows + first_row - block_rows + reaches
        allowed = (key_pos[None, :] <= query_pos[:, None]) & (
            segment_ids(query_pos, doc_starts)[:, None] == segment_ids(key_pos, doc_starts)[None, :]
        )
        scores = (
            jnp.einsum("qkgd,skd->kgqs", query_rows, key_rows, preferred_element_type=jnp.float32)
            * scaling
        )
        scores = jnp.where(allowed[None, None], scores, -jnp.inf)
        return (query_rows, key_rows, value_rows, scores)

    def forward_tile(tile_number):
        query_rows, key_rows, value_rows, scores = tile_scores(tile_number)
        peak_score = jnp.max(scores, axis=-1, keepdims=True)
        log_total = peak_score + jnp.log(
            jnp.sum(jnp.exp(scores - peak_score), axis=-1, keepdims=True)
        )
        weights_bf = jnp.exp(scores - log_total).astype(jnp.bfloat16)
        attended_rows = jnp.einsum(
            "kgqs,skd->qkgd", weights_bf, value_rows, preferred_element_type=jnp.float32
        )
        return (
            attended_rows.astype(jnp.bfloat16).reshape(tile_rows, width_local),
            log_total[..., 0],
        )

    tile_numbers = jnp.arange(tile_count, dtype=jnp.int32)
    attended_tiles, log_totals = lax.map(forward_tile, tile_numbers)
    attended_heads = attended_tiles.reshape(block_rows, width_local)
    grad_heads = lax.all_to_all(grad_out, "head", split_axis=1, concat_axis=0, tiled=True)

    def backward_tile(carry_sums, inputs):
        tile_number, log_total = inputs
        query_rows, key_rows, value_rows, scores = tile_scores(tile_number)
        first_row = tile_number * tile_rows
        grad_rows = lax.dynamic_slice_in_dim(grad_heads, first_row, tile_rows, 0).reshape(
            tile_rows, kv_local, groups, HEAD_DIM
        )
        output_rows = lax.dynamic_slice_in_dim(attended_heads, first_row, tile_rows, 0).reshape(
            tile_rows, kv_local, groups, HEAD_DIM
        )
        row_delta = jnp.einsum(
            "qkgd,qkgd->kgq", grad_rows, output_rows, preferred_element_type=jnp.float32
        )
        weights = jnp.exp(scores - log_total[..., None])
        weights_bf = weights.astype(jnp.bfloat16)
        value_part = jnp.einsum(
            "kgqs,qkgd->skd", weights_bf, grad_rows, preferred_element_type=jnp.float32
        )
        grad_weights = jnp.einsum(
            "qkgd,skd->kgqs", grad_rows, value_rows, preferred_element_type=jnp.float32
        )
        grad_scores = (weights * (grad_weights - row_delta[..., None])).astype(jnp.bfloat16)
        grad_query_rows = (
            jnp.einsum("kgqs,skd->qkgd", grad_scores, key_rows, preferred_element_type=jnp.float32)
            * scaling
        ).astype(jnp.bfloat16)
        key_part = (
            jnp.einsum(
                "kgqs,qkgd->skd", grad_scores, query_rows, preferred_element_type=jnp.float32
            )
            * scaling
        )
        partial_value = jnp.concatenate(
            [key_part.reshape(span_rows, pair_width), value_part.reshape(span_rows, pair_width)],
            axis=1,
        )
        current = lax.dynamic_slice_in_dim(carry_sums, first_row, span_rows, 0)
        carry_sums = lax.dynamic_update_slice_in_dim(
            carry_sums, current + partial_value, first_row, 0
        )
        return (carry_sums, grad_query_rows.reshape(tile_rows, width_local))

    start_sums = jnp.zeros((2 * block_rows, 2 * pair_width), jnp.float32)
    totals, grad_tiles = lax.scan(backward_tile, start_sums, (tile_numbers, log_totals))
    returned = passed_along(totals[:block_rows].astype(jnp.bfloat16), "blk", -1).astype(jnp.float32)
    own_sums = totals[block_rows:] + returned
    grad_key_heads = own_sums[:, :pair_width].astype(jnp.bfloat16)
    grad_value_heads = own_sums[:, pair_width:].astype(jnp.bfloat16)
    grad_query_heads = grad_tiles.reshape(block_rows, width_local)
    attended, grad_query, grad_key, grad_value = (
        lax.all_to_all(attended_heads, "head", split_axis=0, concat_axis=1, tiled=True),
        lax.all_to_all(grad_query_heads, "head", split_axis=0, concat_axis=1, tiled=True),
        lax.all_to_all(grad_key_heads, "head", split_axis=0, concat_axis=1, tiled=True),
        lax.all_to_all(grad_value_heads, "head", split_axis=0, concat_axis=1, tiled=True),
    )
    return (attended, grad_query, grad_key, grad_value)


def solution(mesh):
    in_specs = (
        P(("blk", "head"), None),
        P(("blk", "head"), None),
        P(("blk", "head"), None),
        P(("blk", "head"), None),
        P(),
    )
    out_specs = (
        P(("blk", "head"), None),
        P(("blk", "head"), None),
        P(("blk", "head"), None),
        P(("blk", "head"), None),
    )
    return jax.shard_map(
        per_device, mesh=mesh, in_specs=in_specs, out_specs=out_specs, check_vma=False
    )
```

profile of v0, /device:TPU:0, one launch (start us, length us, event | category | flops | bytes accessed | tf_op | source)
XLA Modules:
  0.0 138.0 jit_solution(2253287352082950581)
XLA Ops:
  0.6 1.8 %copy.93 = bf16[128,1024]{0,1:T(8,128)(2,1)} copy(bf16[128,1024]{1,0:T(8,128)(2,1)} %param.6) | data formatting | bytes 524288 | tf_op args[1]
  2.4 4.2 %all-to-all-start = ((bf16[128,2,512]{0,2,1:T(8,128)(2,1)}), bf16[128,2,512]{0,2,1:T(8,128)(2,1)S(1)}, u32[]{:S(2)}, u32[]{:S(2)}) async-start(bf16[128,2,512]{0,2,1:T(8,128)(2,1)} %bitcast.2), calls=%async_computation | async-start | bytes 524288 | tf_op jit(solution)/shard_map/all_to_all | solution.py:23
  6.7 0.7 copy.97
  7.4 0.1 reduce-window.9
  7.5 0.1 reduce.1
  7.6 0.7 sub.66
  8.2 1.8 %copy.95 = bf16[128,1024]{0,1:T(8,128)(2,1)} copy(bf16[128,1024]{1,0:T(8,128)(2,1)} %param.7) | data formatting | bytes 524288 | tf_op args[2]
  10.0 2.3 %copy.150 = bf16[16,2,8,2048]{3,2,0,1:T(8,128)(2,1)} copy(bf16[16,2,8,2048]{3,2,1,0:T(8,128)(2,1)} %bitcast.127) | data formatting | bytes 2097152 | tf_op jit(solution)/shard_map/all_to_all | solution.py:22
  12.3 0.1 convert_reduce_fusion.1
  12.4 0.1 all-to-all-done
  12.5 3.4 %all-to-all-start.1 = ((bf16[128,2,512]{0,2,1:T(8,128)(2,1)}), bf16[128,2,512]{0,2,1:T(8,128)(2,1)S(1)}, u32[]{:S(2)}, u32[]{:S(2)}) async-start(bf16[128,2,512]{0,2,1:T(8,128)(2,1)} %bitcast.4), calls=%async_computation.1 | async-start | bytes 524288 | tf_op jit(solution)/shard_map/all_to_all | solution.py:24
  16.0 5.8 %all-to-all-done.1 = bf16[128,2,512]{0,2,1:T(8,128)(2,1)S(1)} async-done(((bf16[128,2,512]{0,2,1:T(8,128)(2,1)}), bf16[128,2,512]{0,2,1:T(8,128)(2,1)S(1)}, u32[]{:S(2)}, u32[]{:S(2)}) %all-to-all-start.1) | async-done | bytes 262176 | tf_op jit(solution)/shard_map/all_to_all | solution.py:24
  21.8 3.6 %all-to-all-start.2 = ((bf16[128,2,2048]{2,0,1:T(8,128)(2,1)}), bf16[128,2,2048]{2,0,1:T(8,128)(2,1)S(1)}, u32[]{:S(2)}, u32[]{:S(2)}) async-start(bf16[128,2,2048]{2,0,1:T(8,128)(2,1)} %bitcast.114), calls=%async_computation.2 | async-start | bytes 2097152 | tf_op jit(solution)/shard_map/all_to_all | solution.py:22
  25.4 2.3 %copy.149 = bf16[16,2,8,2048]{3,2,0,1:T(8,128)(2,1)} copy(bf16[16,2,8,2048]{3,2,1,0:T(8,128)(2,1)} %bitcast.128) | data formatting | bytes 2097152 | tf_op jit(solution)/shard_map/all_to_all | solution.py:81
  27.7 0.7 bitcast_dynamic-update-slice_fusion.1
  28.4 0.7 bitcast_dynamic-update-slice_fusion
  29.1 2.1 %collective-permute-start = (bf16[256,1024]{0,1:T(8,128)(2,1)}, bf16[256,1024]{0,1:T(8,128)(2,1)}, u32[]{:S(2)}, u32[]{:S(2)}) collective-permute-start(bf16[256,1024]{0,1:T(8,128)(2,1)} %bitcast_dynamic-update-slice_fusion), channel_id=1, source_target_pairs={{0,2},{2,4},{4,6},{6,8},{8,10},{10,12},{12,14},{14,16},{16,18},{18... | collective-permute-start | bytes 1572872 | tf_op jit(solution)/shard_map/ppermute | solution.py:12
  31.2 7.4 %all-to-all-done.2 = bf16[128,2,2048]{2,0,1:T(8,128)(2,1)S(1)} async-done(((bf16[128,2,2048]{2,0,1:T(8,128)(2,1)}), bf16[128,2,2048]{2,0,1:T(8,128)(2,1)S(1)}, u32[]{:S(2)}, u32[]{:S(2)}) %all-to-all-start.2) | async-done | bytes 1048608 | tf_op jit(solution)/shard_map/all_to_all | solution.py:22
  38.6 3.6 %all-to-all-start.4 = ((bf16[128,2,2048]{2,0,1:T(8,128)(2,1)}), bf16[128,2,2048]{2,0,1:T(8,128)(2,1)S(1)}, u32[]{:S(2)}, u32[]{:S(2)}) async-start(bf16[128,2,2048]{2,0,1:T(8,128)(2,1)} %bitcast.113), calls=%async_computation.4 | async-start | bytes 2097152 | tf_op jit(solution)/shard_map/all_to_all | solution.py:81
  42.2 0.1 convert_reduce_fusion
  42.3 0.2 compare_and_fusion
  42.5 0.8 reshape.198
  43.3 0.8 copy.109
  44.1 10.5 %all-to-all-done.4 = bf16[128,2,2048]{2,0,1:T(8,128)(2,1)S(1)} async-done(((bf16[128,2,2048]{2,0,1:T(8,128)(2,1)}), bf16[128,2,2048]{2,0,1:T(8,128)(2,1)S(1)}, u32[]{:S(2)}, u32[]{:S(2)}) %all-to-all-start.4) | async-done | bytes 1048608 | tf_op jit(solution)/shard_map/all_to_all | solution.py:81
  54.6 0.7 reshape.199
  55.4 1.6 %copy.111 = bf16[256,4,4,128]{0,3,2,1:T(8,128)(2,1)} copy(bf16[256,4,4,128]{3,2,1,0:T(4,128)(2,1)S(1)} %reshape.199) | data formatting | bytes 2097152 | tf_op jit(solution)/shard_map/while/body/eval_jaxpr/reshape | solution.py:87
  57.0 0.0 collective-permute-done
  57.0 1.3 pad_maximum_fusion.1
  58.3 1.4 %fusion.3 = (f32[4,4,256]{2,1,0:T(4,128)S(1)}, f32[4,512,256,4]{2,1,3,0:T(8,128)S(1)}) fusion(pred[256,512]{0,1:T(8,128)(4,1)S(1)} %compare_and_fusion, bf16[512,4,128,1]{0,2,3,1:T(8,128)(2,1)S(1)} %bitcast.120, bf16[256,4,4,128]{0,3,2,1:T(8,128)(2,1)S(1)} %copy.109), kind=kOutput, calls=%fused_computation.7 | convolution fusion | flops 543158272 | bytes 10108928 | tf_op jit(solution)/shard_map/while/body/eval_jaxpr/qkgd,skd->kgqs/dot_general | solution.py:57
  59.7 1.7 %exponential_reduce_fusion = f32[4,4,256]{2,1,0:T(4,128)S(1)} fusion(f32[4,512,256,4]{2,1,3,0:T(8,128)S(1)} %get-tuple-element.84, f32[4,4,256]{2,1,0:T(4,128)S(1)} %get-tuple-element.71, pred[256,512]{0,1:T(8,128)(4,1)S(1)} %compare_and_fusion), kind=kLoop, calls=%fused_computation.5 | loop fusion | flops 8384512 | bytes 8552448 | tf_op jit(solution)/shard_map/while/body/eval_jaxpr/reduce_sum | solution.py:67
  61.4 4.0 %bitcast_convert_fusion = (f32[4,4,256,128]{2,3,1,0:T(8,128)}, bf16[4,128,4,256]{3,1,2,0:T(8,128)(2,1)}) fusion(bf16[512,4,128,1]{0,2,3,1:T(8,128)(2,1)S(1)} %bitcast.132, f32[4,512,256,4]{2,1,3,0:T(8,128)S(1)} %get-tuple-element.84, f32[4,4,256]{2,1,0:T(4,128)S(1)} %bitcast.136, pred[256,512]{0,1:T(8,128)(4,1)S(1)} %compare_and_fusion), kind=kOutput, calls=%fused_computation.25 | convolution fusion | flops 546308096 | bytes 12206080 | tf_op jit(solution)/shard_map/while/body/eval_jaxpr/kgqs,skd->qkgd/dot_general | solution.py:70
  65.3 0.0 copy-done
  65.4 3.1 %copy.129 = f32[4,4,256,128]{3,1,0,2:T(4,128)} copy(f32[4,4,256,128]{2,3,1,0:T(8,128)} %get-tuple-element.85) | data formatting | bytes 4194304
  68.4 2.9 %multiply_reduce_fusion = f32[4,4,256]{1,0,2:T(4,128)S(1)} fusion(f32[4,4,256,128]{3,1,0,2:T(4,128)} %copy.129, bf16[256,4,4,128]{3,2,1,0:T(4,128)(2,1)S(1)} %reshape.199), kind=kLoop, calls=%fused_computation.10 | loop fusion | flops 1568768 | bytes 3162112
  71.3 0.0 copy-start.2
  71.3 0.2 copy.130
  71.5 7.0 %fusion.11 = f32[4,512,128,1]{1,2,3,0:T(8,128)} fusion(bf16[256,4,4,128]{0,3,2,1:T(8,128)(2,1)} %copy.111, f32[4,512,256,4]{2,1,3,0:T(8,128)} %copy-done, f32[4,4,256]{2,1,0:T(4,128)S(1)} %bitcast.137, pred[256,512]{0,1:T(8,128)(4,1)S(1)} %compare_and_fusion), kind=kOutput, calls=%fused_computation.32 | convolution fusion | flops 545259520 | bytes 10633216 | tf_op jit(solution)/shard_map/while/body/eval_jaxpr/kgqs,qkgd->skd/dot_general | solution.py:98
  78.5 5.1 %fusion.1 = bf16[4,4,256,512]{2,3,1,0:T(8,128)(2,1)S(1)} fusion(f32[4,512,256,4]{2,1,3,0:T(8,128)} %copy-done, f32[4,4,256]{2,1,0:T(4,128)S(1)} %copy.130, f32[4,4,256]{2,1,0:T(4,128)S(1)} %bitcast.138, pred[256,512]{0,1:T(8,128)(4,1)S(1)} %compare_and_fusion, bf16[512,4,128,1]{0,2,3,1:T(8,128)(2,1)S(1)} %bitcast.133, bf16[256,4,4,128]{0,3,2,1:T(8,128)(2,1)S(1)} %copy-done.2), kind=kOutput, calls=%fused_computation.2 | convolution fusion | flops 549453824 | bytes 14319616 | tf_op jit(solution)/shard_map/while/body/eval_jaxpr/qkgd,skd->kgqs/dot_general | solution.py:101
  83.6 1.5 %fusion.5 = f32[4,512,128]{1,2,0:T(8,128)S(1)} fusion(bf16[4,4,256,512]{2,3,1,0:T(8,128)(2,1)S(1)} %fusion.1, bf16[256,4,4,128]{0,3,2,1:T(8,128)(2,1)S(1)} %copy.109), kind=kOutput, calls=%fused_computation.15 | convolution fusion | flops 537133056 | bytes 6291456 | tf_op jit(solution)/shard_map/while/body/eval_jaxpr/kgqs,qkgd->skd/dot_general | solution.py:110
  85.1 1.7 %fusion.4 = bf16[256,4,4,128]{0,3,2,1:T(8,128)(2,1)} fusion(bf16[512,4,128,1]{0,2,3,1:T(8,128)(2,1)S(1)} %bitcast.121, bf16[4,4,256,512]{2,3,1,0:T(8,128)(2,1)S(1)} %fusion.1), kind=kOutput, calls=%fused_computation.13 | convolution fusion | flops 537919488 | bytes 5767168 | tf_op jit(solution)/shard_map/while/body/eval_jaxpr/kgqs,skd->qkgd/dot_general | solution.py:106
  86.8 1.3 all_to_all.126
  88.2 1.1 copy.107
  89.3 3.6 %all-to-all-start.5 = ((bf16[2,128,2048]{1,2,0:T(8,128)(2,1)}), bf16[2,128,2048]{1,2,0:T(8,128)(2,1)S(1)}, u32[]{:S(2)}, u32[]{:S(2)}) async-start(bf16[2,128,2048]{1,2,0:T(8,128)(2,1)} %copy.107), calls=%async_computation.5 | async-start | bytes 2097152 | tf_op jit(solution)/shard_map/all_to_all | solution.py:134
  92.9 0.9 fusion.9
  93.7 1.3 collective-permute-start.1
  95.0 2.1 %all_to_all.119 = bf16[2,128,2048]{1,0,2:T(2,128)(2,1)} reshape(bf16[256,4,4,128]{0,3,2,1:T(8,128)(2,1)} %bitcast.129) | data formatting | bytes 2097152 | tf_op jit(solution)/shard_map/all_to_all | solution.py:133
  97.2 2.3 %copy.102 = bf16[2,128,2048]{1,2,0:T(8,128)(2,1)} copy(bf16[2,128,2048]{1,0,2:T(2,128)(2,1)} %all_to_all.119) | data formatting | bytes 2097152 | tf_op jit(solution)/shard_map/all_to_all | solution.py:133
  99.5 5.0 %all-to-all-done.5 = bf16[2,128,2048]{1,2,0:T(8,128)(2,1)S(1)} async-done(((bf16[2,128,2048]{1,2,0:T(8,128)(2,1)}), bf16[2,128,2048]{1,2,0:T(8,128)(2,1)S(1)}, u32[]{:S(2)}, u32[]{:S(2)}) %all-to-all-start.5) | async-done | bytes 1048608 | tf_op jit(solution)/shard_map/all_to_all | solution.py:134
  104.5 4.4 %all-to-all-start.3 = ((bf16[2,128,2048]{1,2,0:T(8,128)(2,1)}), bf16[2,128,2048]{1,2,0:T(8,128)(2,1)}, u32[]{:S(2)}, u32[]{:S(2)}) async-start(bf16[2,128,2048]{1,2,0:T(8,128)(2,1)} %copy.102), calls=%async_computation.3 | async-start | bytes 2097152 | tf_op jit(solution)/shard_map/all_to_all | solution.py:133
  108.9 0.0 collective-permute-done.1
  108.9 1.2 fusion.8
  110.2 0.8 copy.112
  111.0 8.7 %all-to-all-done.3 = bf16[2,128,2048]{1,2,0:T(8,128)(2,1)} async-done(((bf16[2,128,2048]{1,2,0:T(8,128)(2,1)}), bf16[2,128,2048]{1,2,0:T(8,128)(2,1)}, u32[]{:S(2)}, u32[]{:S(2)}) %all-to-all-start.3) | async-done | bytes 1048608 | tf_op jit(solution)/shard_map/all_to_all | solution.py:133
  119.7 3.4 %all-to-all-start.6 = ((bf16[2,128,512]{2,1,0:T(8,128)(2,1)}), bf16[2,128,512]{2,1,0:T(8,128)(2,1)S(1)}, u32[]{:S(2)}, u32[]{:S(2)}) async-start(bf16[2,128,512]{2,1,0:T(8,128)(2,1)} %bitcast.34), calls=%async_computation.6 | async-start | bytes 524288 | tf_op jit(solution)/shard_map/all_to_all | solution.py:135
  123.2 0.8 copy.114
  124.0 4.3 %all-to-all-done.6 = bf16[2,128,512]{2,1,0:T(8,128)(2,1)S(1)} async-done(((bf16[2,128,512]{2,1,0:T(8,128)(2,1)}), bf16[2,128,512]{2,1,0:T(8,128)(2,1)S(1)}, u32[]{:S(2)}, u32[]{:S(2)}) %all-to-all-start.6) | async-done | bytes 262176 | tf_op jit(solution)/shard_map/all_to_all | solution.py:135
  128.3 3.4 %all-to-all-start.7 = ((bf16[2,128,512]{2,1,0:T(8,128)(2,1)}), bf16[2,128,512]{2,1,0:T(8,128)(2,1)S(1)}, u32[]{:S(2)}, u32[]{:S(2)}) async-start(bf16[2,128,512]{2,1,0:T(8,128)(2,1)} %bitcast.37), calls=%async_computation.7 | async-start | bytes 524288 | tf_op jit(solution)/shard_map/all_to_all | solution.py:136
  131.8 1.3 copy.117
  133.1 2.3 %copy.116 = bf16[128,4096]{1,0:T(8,128)(2,1)} copy(bf16[128,4096]{0,1:T(8,128)(2,1)} %bitcast.16) | data formatting | bytes 2097152
  135.3 0.2 copy.113
  135.5 0.9 copy.118
  136.4 0.6 all-to-all-done.7
  136.9 0.2 copy.115
  137.1 0.9 copy.119
  (14 shorter events, 0.1 us)
Async XLA Ops:
  2.4 10.1 %all-to-all-start = ((bf16[128,2,512]{0,2,1:T(8,128)(2,1)}), bf16[128,2,512]{0,2,1:T(8,128)(2,1)S(1)}, u32[]{:S(2)}, u32[]{:S(2)}) async-start(bf16[128,2,512]{0,2,1:T(8,128)(2,1)} %bitcast.2), calls=%async_computation | async-start | bytes 524288 | tf_op jit(solution)/shard_map/all_to_all | solution.py:23
  12.5 9.2 %all-to-all-start.1 = ((bf16[128,2,512]{0,2,1:T(8,128)(2,1)}), bf16[128,2,512]{0,2,1:T(8,128)(2,1)S(1)}, u32[]{:S(2)}, u32[]{:S(2)}) async-start(bf16[128,2,512]{0,2,1:T(8,128)(2,1)} %bitcast.4), calls=%async_computation.1 | async-start | bytes 524288 | tf_op jit(solution)/shard_map/all_to_all | solution.py:24
  21.8 16.9 %all-to-all-start.2 = ((bf16[128,2,2048]{2,0,1:T(8,128)(2,1)}), bf16[128,2,2048]{2,0,1:T(8,128)(2,1)S(1)}, u32[]{:S(2)}, u32[]{:S(2)}) async-start(bf16[128,2,2048]{2,0,1:T(8,128)(2,1)} %bitcast.114), calls=%async_computation.2 | async-start | bytes 2097152 | tf_op jit(solution)/shard_map/all_to_all | solution.py:22
  29.1 27.8 %collective-permute-start = (bf16[256,1024]{0,1:T(8,128)(2,1)}, bf16[256,1024]{0,1:T(8,128)(2,1)}, u32[]{:S(2)}, u32[]{:S(2)}) collective-permute-start(bf16[256,1024]{0,1:T(8,128)(2,1)} %bitcast_dynamic-update-slice_fusion), channel_id=1, source_target_pairs={{0,2},{2,4},{4,6},{6,8},{8,10},{10,12},{12,14},{14,16},{16,18},{18... | collective-permute-start | bytes 1572872 | tf_op jit(solution)/shard_map/ppermute | solution.py:12
  38.6 16.0 %all-to-all-start.4 = ((bf16[128,2,2048]{2,0,1:T(8,128)(2,1)}), bf16[128,2,2048]{2,0,1:T(8,128)(2,1)S(1)}, u32[]{:S(2)}, u32[]{:S(2)}) async-start(bf16[128,2,2048]{2,0,1:T(8,128)(2,1)} %bitcast.113), calls=%async_computation.4 | async-start | bytes 2097152 | tf_op jit(solution)/shard_map/all_to_all | solution.py:81
  58.2 3.1 %copy-start.3 = (bf16[512,512]{0,1:T(8,128)(2,1)}, bf16[512,512]{0,1:T(8,128)(2,1)S(1)}, u32[]{:S(2)}) copy-start(bf16[512,512]{0,1:T(8,128)(2,1)S(1)} %get-tuple-element.68) | copy-start | bytes 1572868
  59.6 5.7 %copy-start = (f32[4,512,256,4]{2,1,3,0:T(8,128)}, f32[4,512,256,4]{2,1,3,0:T(8,128)S(1)}, u32[]{:S(2)}) copy-start(f32[4,512,256,4]{2,1,3,0:T(8,128)S(1)} %get-tuple-element.84) | copy-start | bytes 25165828
  71.3 7.2 %copy-start.2 = (bf16[256,4,4,128]{0,3,2,1:T(8,128)(2,1)S(1)}, bf16[256,4,4,128]{0,3,2,1:T(8,128)(2,1)}, u32[]{:S(2)}) copy-start(bf16[256,4,4,128]{0,3,2,1:T(8,128)(2,1)} %copy.111) | copy-start | bytes 3145732
  71.5 7.0 %copy-start.4 = (bf16[512,512]{0,1:T(8,128)(2,1)S(1)}, bf16[512,512]{0,1:T(8,128)(2,1)}, u32[]{:S(2)}) copy-start(bf16[512,512]{0,1:T(8,128)(2,1)} %copy-done.3) | copy-start | bytes 1572868
  85.1 7.8 %copy-start.1 = (f32[4,512,128,1]{1,2,3,0:T(8,128)S(1)}, f32[4,512,128,1]{1,2,3,0:T(8,128)}, u32[]{:S(2)}) copy-start(f32[4,512,128,1]{1,2,3,0:T(8,128)} %fusion.11) | copy-start | bytes 3145732
  89.3 15.2 %all-to-all-start.5 = ((bf16[2,128,2048]{1,2,0:T(8,128)(2,1)}), bf16[2,128,2048]{1,2,0:T(8,128)(2,1)S(1)}, u32[]{:S(2)}, u32[]{:S(2)}) async-start(bf16[2,128,2048]{1,2,0:T(8,128)(2,1)} %copy.107), calls=%async_computation.5 | async-start | bytes 2097152 | tf_op jit(solution)/shard_map/all_to_all | solution.py:134
  93.7 15.1 %collective-permute-start.1 = (bf16[256,1024]{0,1:T(8,128)(2,1)}, bf16[256,1024]{0,1:T(8,128)(2,1)}, u32[]{:S(2)}, u32[]{:S(2)}) collective-permute-start(bf16[256,1024]{0,1:T(8,128)(2,1)} %fusion.9), channel_id=1, source_target_pairs={{2,0},{4,2},{6,4},{8,6},{10,8},{12,10},{14,12},{16,14},{18,16},{20... | collective-permute-start | bytes 1572872 | tf_op jit(solution)/shard_map/ppermute | solution.py:12
  104.5 15.3 %all-to-all-start.3 = ((bf16[2,128,2048]{1,2,0:T(8,128)(2,1)}), bf16[2,128,2048]{1,2,0:T(8,128)(2,1)}, u32[]{:S(2)}, u32[]{:S(2)}) async-start(bf16[2,128,2048]{1,2,0:T(8,128)(2,1)} %copy.102), calls=%async_computation.3 | async-start | bytes 2097152 | tf_op jit(solution)/shard_map/all_to_all | solution.py:133
  119.7 8.6 %all-to-all-start.6 = ((bf16[2,128,512]{2,1,0:T(8,128)(2,1)}), bf16[2,128,512]{2,1,0:T(8,128)(2,1)S(1)}, u32[]{:S(2)}, u32[]{:S(2)}) async-start(bf16[2,128,512]{2,1,0:T(8,128)(2,1)} %bitcast.34), calls=%async_computation.6 | async-start | bytes 524288 | tf_op jit(solution)/shard_map/all_to_all | solution.py:135
  128.3 8.6 %all-to-all-start.7 = ((bf16[2,128,512]{2,1,0:T(8,128)(2,1)}), bf16[2,128,512]{2,1,0:T(8,128)(2,1)S(1)}, u32[]{:S(2)}, u32[]{:S(2)}) async-start(bf16[2,128,512]{2,1,0:T(8,128)(2,1)} %bitcast.37), calls=%async_computation.7 | async-start | bytes 524288 | tf_op jit(solution)/shard_map/all_to_all | solution.py:136
where the time goes:
time: 139 us; the launch traced here: 138 us
  waiting for transfers between devices  42.4 us (31%)
  starting transfers between devices  33.1 us (24%)
  local copies, waits for them, and re-layouts  31.8 us (23%)
  matrix products  20.6 us (15%)
  other arithmetic  9.22 us (7%)
    unnamed x18, local copies, waits for them, and re-layouts  12.7 us
    all_to_all x1, waiting for transfers between devices, per_device(): lax.all_to_all(grad_out, 'head', split_axis=1, concat_axis=0, tiled=True)  10.5 us
    all_to_all x1, waiting for transfers between devices, per_device(): lax.all_to_all(attended_heads, 'head', split_axis=0, concat_axis=1, tiled...  8.71 us
    all_to_all x1, waiting for transfers between devices, per_device(): lax.all_to_all(query, 'head', split_axis=1, concat_axis=0, tiled=True)  7.42 us
    dot_general x1, matrix products, backward_tile(): jnp.einsum('kgqs,qkgd->skd', weights_bf, grad_rows, preferred_element_typ...  6.98 us
    all_to_all x1, waiting for transfers between devices, per_device(): lax.all_to_all(value, 'head', split_axis=1, concat_axis=0, tiled=True)  5.77 us
    dot_general x1, matrix products, backward_tile(): jnp.einsum('qkgd,skd->kgqs', grad_rows, value_rows, preferred_element_typ...  5.1 us
    all_to_all x1, waiting for transfers between devices, per_device(): lax.all_to_all(grad_query_heads, 'head', split_axis=0, concat_axis=1, til...  4.96 us
  transfers between devices with their start and end apart: 10, of which 8 were waited for; matrix products, arithmetic and copies ran while one was open for 18% of the time, Pallas kernels for 0%

commit v1 on v0

v1 whole, which is shorter than its diff:
```python
import functools
import math

import jax
import jax.numpy as jnp
from jax import lax
from jax.experimental import pallas as pl
from jax.experimental.pallas import tpu as pltpu
from jax.sharding import PartitionSpec as P

HEAD_DIM = 128
EXCLUDED = -1e30
MESH = pl.DeviceIdType.MESH


def kernel(
    back, total, lens, q_hbm, k_hbm, v_hbm, do_hbm, att_hbm, dq_hbm, dk_hbm, dv_hbm,
    window, qbuf, dobuf, attbuf, dqbuf, part, landed, own, summed, bias,
    kv_in, q_in, out_sem, sum_sem, kv_send, kv_recv, g_send, g_recv,
):
    rows = q_hbm.shape[0]
    kv_heads = k_hbm.shape[1] // HEAD_DIM
    groups = q_hbm.shape[1] // k_hbm.shape[1]
    width = groups * HEAD_DIM
    span = (back + 1) * rows
    scaling = HEAD_DIM ** (-0.5)
    me = lax.axis_index("blk") * back + lax.axis_index("head")

    def device(number):
        return {"blk": number // back, "head": number % back}

    def columns(g, size):
        return pl.ds(pl.multiple_of(g * size, size), size)

    def slot(k):
        return pl.ds((back - k) * rows, rows)

    def kv_load(g, which):
        return pltpu.make_async_copy(
            (k_hbm, v_hbm)[which].at[:, columns(g, HEAD_DIM)],
            window.at[g, which, slot(0), :],
            kv_in.at[which, g],
        )

    def q_load(g, which):
        return pltpu.make_async_copy(
            (q_hbm, do_hbm)[which].at[:, columns(g, width)],
            (qbuf, dobuf)[which].at[g],
            q_in.at[which, g],
        )

    def result(g, which):
        return pltpu.make_async_copy(
            (attbuf, dqbuf)[which].at[g],
            (att_hbm, dq_hbm)[which].at[:, columns(g, width)],
            out_sem.at[which, g],
        )

    def sum_result(g, which):
        return pltpu.make_async_copy(
            summed.at[g, which],
            (dk_hbm, dv_hbm)[which].at[:, columns(g, HEAD_DIM)],
            sum_sem.at[which, g],
        )

    def kv_copy(g, k):
        return pltpu.make_async_remote_copy(
            src_ref=window.at[g, :, slot(0), :],
            dst_ref=window.at[g, :, slot(k), :],
            send_sem=kv_send.at[k - 1, g],
            recv_sem=kv_recv.at[k - 1, g],
            device_id=device(me + k),
            device_id_type=MESH,
        )

    def g_copy(g, k):
        return pltpu.make_async_remote_copy(
            src_ref=part.at[g, :, slot(k), :],
            dst_ref=landed.at[g, k - 1],
            send_sem=g_send.at[k - 1, g],
            recv_sem=g_recv.at[k - 1, g],
            device_id=device(me - k),
            device_id_type=MESH,
        )

    @pl.loop(0, kv_heads)
    def _(g):
        kv_load(g, 0).start()
        kv_load(g, 1).start()

    barrier = pltpu.get_barrier_semaphore()
    for k in range(1, back + 1):
        @pl.when(me + k < total)
        def _():
            pl.semaphore_signal(barrier, inc=1, device_id=device(me + k), device_id_type=MESH)

        @pl.when(me - k >= 0)
        def _():
            pl.semaphore_signal(barrier, inc=1, device_id=device(me - k), device_id_type=MESH)

    @pl.loop(0, kv_heads)
    def _(g):
        q_load(g, 0).start()
        q_load(g, 1).start()

    greeted = jnp.minimum(me, back) + jnp.minimum(total - 1 - me, back)
    pl.semaphore_wait(barrier, greeted)

    @pl.loop(0, kv_heads)
    def _(g):
        kv_load(g, 0).wait()
        kv_load(g, 1).wait()
        for k in range(1, back + 1):
            @pl.when(me + k < total)
            def _():
                kv_copy(g, k).start()

    for k in range(1, back + 1):
        @pl.when(me - k < 0)
        def _():
            window[:, :, slot(k), :] = jnp.zeros((kv_heads, 2, rows, HEAD_DIM), jnp.bfloat16)

        @pl.when(me + k >= total)
        def _():
            landed[:, k - 1] = jnp.zeros((kv_heads, 2, rows, HEAD_DIM), jnp.bfloat16)

    query_pos = me * rows + lax.broadcasted_iota(jnp.int32, (1, rows), 1)

    def latest(d, carry):
        start, first = carry
        return start + lens[d], jnp.where(query_pos >= start, start, first)

    _, first = lax.fori_loop(
        0, lens.shape[0], latest, (jnp.int32(0), jnp.zeros((1, rows), jnp.int32))
    )
    key_pos = (me - back) * rows + lax.broadcasted_iota(jnp.int32, (span, rows), 0)
    bias[...] = jnp.where((key_pos <= query_pos) & (key_pos >= first), 0.0, EXCLUDED)

    def dot(a, b, a_dim, b_dim):
        return lax.dot_general(
            a, b, (((a_dim,), (b_dim,)), ((), ())), preferred_element_type=jnp.float32
        )

    def stacked(values):
        return jnp.concatenate(
            [values[:, h * HEAD_DIM : (h + 1) * HEAD_DIM] for h in range(groups)], axis=0
        )

    @pl.loop(0, kv_heads)
    def _(g):
        q_load(g, 0).wait()
        q_load(g, 1).wait()
        for k in range(1, back + 1):
            @pl.when(me - k >= 0)
            def _():
                kv_copy(g, k).wait_recv()

        keys, values = window[g, 0], window[g, 1]
        queries, grads = stacked(qbuf[g]), stacked(dobuf[g])
        kept = jnp.concatenate([bias[...]] * groups, axis=1)
        scores = dot(keys, queries, 1, 1) * (scaling * math.log2(math.e)) + kept
        peak = jnp.max(scores, axis=0, keepdims=True)
        raised = jnp.exp2(scores - peak)
        weights = raised * (1.0 / jnp.sum(raised, axis=0, keepdims=True))
        weights_bf = weights.astype(jnp.bfloat16)
        attended = dot(values, weights_bf, 0, 0)
        grad_weights = dot(values, grads, 1, 1)
        delta = jnp.sum(weights * grad_weights, axis=0, keepdims=True)
        grad_scores = (weights * (grad_weights - delta)).astype(jnp.bfloat16)
        grad_query = dot(keys, grad_scores, 0, 0) * scaling
        grad_key = dot(grad_scores, queries, 1, 0) * scaling
        grad_value = dot(weights_bf, grads, 1, 0)
        part[g, 0] = grad_key[: back * rows].astype(jnp.bfloat16)
        part[g, 1] = grad_value[: back * rows].astype(jnp.bfloat16)
        own[g, 0] = grad_key[back * rows :]
        own[g, 1] = grad_value[back * rows :]
        for h in range(groups):
            at = slice(h * HEAD_DIM, (h + 1) * HEAD_DIM)
            attbuf[g, :, at] = attended[:, at].T.astype(jnp.bfloat16)
            dqbuf[g, :, at] = grad_query[:, at].T.astype(jnp.bfloat16)
        for k in range(1, back + 1):
            @pl.when(me - k >= 0)
            def _():
                g_copy(g, k).start()
        result(g, 0).start()
        result(g, 1).start()

    @pl.loop(0, kv_heads)
    def _(g):
        for k in range(1, back + 1):
            @pl.when(me + k < total)
            def _():
                g_copy(g, k).wait_recv()
        sums = own[g]
        for k in range(1, back + 1):
            sums = sums + landed[g, k - 1].astype(jnp.float32)
        summed[g] = sums.astype(jnp.bfloat16)
        sum_result(g, 0).start()
        sum_result(g, 1).start()

    @pl.loop(0, kv_heads)
    def _(g):
        for k in range(1, back + 1):
            @pl.when(me + k < total)
            def _():
                kv_copy(g, k).wait_send()

            @pl.when(me - k >= 0)
            def _():
                g_copy(g, k).wait_send()
        for which in range(2):
            result(g, which).wait()
            sum_result(g, which).wait()


def solution(mesh):
    back = mesh.shape["head"]
    total = mesh.shape["blk"] * back

    def per_device(query, key, value, grad_out, doc_lengths):
        rows, kv_heads = query.shape[0], key.shape[1] // HEAD_DIM
        width = query.shape[1] // kv_heads
        bf, f32 = jnp.bfloat16, jnp.float32
        anywhere = pl.BlockSpec(memory_space=pl.ANY)
        dma = pltpu.SemaphoreType.DMA
        return pl.pallas_call(
            functools.partial(kernel, back, total),
            out_shape=[
                jax.ShapeDtypeStruct(query.shape, bf),
                jax.ShapeDtypeStruct(query.shape, bf),
                jax.ShapeDtypeStruct(key.shape, bf),
                jax.ShapeDtypeStruct(key.shape, bf),
            ],
            in_specs=[pl.BlockSpec(memory_space=pltpu.SMEM)] + [anywhere] * 4,
            out_specs=[anywhere] * 4,
            scratch_shapes=[
                pltpu.VMEM((kv_heads, 2, (back + 1) * rows, HEAD_DIM), bf),
                pltpu.VMEM((kv_heads, rows, width), bf),
                pltpu.VMEM((kv_heads, rows, width), bf),
                pltpu.VMEM((kv_heads, rows, width), bf),
                pltpu.VMEM((kv_heads, rows, width), bf),
                pltpu.VMEM((kv_heads, 2, back * rows, HEAD_DIM), bf),
                pltpu.VMEM((kv_heads, back, 2, rows, HEAD_DIM), bf),
                pltpu.VMEM((kv_heads, 2, rows, HEAD_DIM), f32),
                pltpu.VMEM((kv_heads, 2, rows, HEAD_DIM), bf),
                pltpu.VMEM(((back + 1) * rows, rows), f32),
                dma((2, kv_heads)),
                dma((2, kv_heads)),
                dma((2, kv_heads)),
                dma((2, kv_heads)),
                dma((back, kv_heads)),
                dma((back, kv_heads)),
                dma((back, kv_heads)),
                dma((back, kv_heads)),
            ],
            compiler_params=pltpu.CompilerParams(collective_id=0, has_side_effects=True),
        )(doc_lengths, query, key, value, grad_out)

    split = P(("blk", "head"), None)
    return jax.shard_map(
        per_device,
        mesh=mesh,
        in_specs=(split, split, split, split, P()),
        out_specs=(split, split, split, split),
        check_vma=False,
    )
```

time: 139 us -> 36 us (0.26)
  waiting for transfers between devices: 42.4 us -> 0 us
  starting transfers between devices: 33.1 us -> 0 us
  Pallas kernels: 0 us -> 30 us
  local copies, waits for them, and re-layouts: 31.8 us -> 5.22 us
  matrix products: 20.6 us -> 0 us
  other arithmetic: 9.22 us -> 0 us
    all_to_all x8 -> x0, waiting for transfers between devices: 42.4 us -> none  [the longest x1 10.5 us: per_device(): lax.all_to_all(grad_out, 'head', split_axis=1, concat_axis=0, tiled=True)]
    pallas_call x0 -> x1, Pallas kernels: none -> 30 us  [per_device(): pl.pallas_call(functools.partial(kernel, back, total), out_shape=[jax.Sha...]
    all_to_all x8 -> x0, starting transfers between devices: 29.7 us -> none  [the longest x1 4.41 us: per_device(): lax.all_to_all(attended_heads, 'head', split_axis=0, concat_axis=1, tiled...]
    dot_general x6 -> x0, matrix products: 20.6 us -> none  [the longest x1 6.98 us: backward_tile(): jnp.einsum('kgqs,qkgd->skd', weights_bf, grad_rows, preferred_element_typ...]
    all_to_all x8 -> x0, local copies, waits for them, and re-layouts: 11.9 us -> none  [the longest x2 4.47 us: per_device(): lax.all_to_all(attended_heads, 'head', split_axis=0, concat_axis=1, tiled...]
    unnamed x18 -> x10, local copies, waits for them, and re-layouts: 12.7 us -> 5.22 us
    reshape x4 -> x0, local copies, waits for them, and re-layouts: 3.87 us -> none  [the longest x2 2.32 us: backward_tile(): lax.dynamic_slice_in_dim(grad_heads, first_row, tile_rows, 0)]
    ppermute x2 -> x0, starting transfers between devices: 3.36 us -> none  [passed_along(): lax.ppermute(value, axis, [(source, source + steps) for source in range(i...]
  transfers between devices with their start and end apart: 10 -> 0, of which waited for: 8 -> 0; matrix products, arithmetic and copies ran while one was open for 18% -> 0% of each run, Pallas kernels for 0% -> 0%
where the time goes in v1:
time: 36 us; the launch traced here: 35.8 us
  Pallas kernels  30 us (83%)
  local copies, waits for them, and re-layouts  5.22 us (14%)
  between operations  0.65 us (2%)
    pallas_call x1, Pallas kernels, per_device(): pl.pallas_call(functools.partial(kernel, back, total), out_shape=[jax.Sha...  30 us
    unnamed x10, local copies, waits for them, and re-layouts  5.22 us

profile of v1, /device:TPU:0, one launch (start us, length us, event | category | flops | bytes accessed | tf_op | source)
XLA Modules:
  0.0 35.8 jit_solution(9182787156455015501)
XLA Ops:
  0.6 30.0 %shard_map.84 = (bf16[128,4096]{1,0:T(8,128)(2,1)}, bf16[128,4096]{1,0:T(8,128)(2,1)}, bf16[128,1024]{1,0:T(8,128)(2,1)}, bf16[128,1024]{1,0:T(8,128)(2,1)}) custom-call(s32[32]{0:T(128)} %lens.1, bf16[128,4096]{1,0:T(8,128)(2,1)} %q_hbm.1, bf16[128,1024]{1,0:T(8,128)(2,1)} %k_hbm.1, bf16[128,1024]{1,0:T(8,128)(2,1)} %v_hbm.1, bf16[128,4096]{1,0:T(8,128)(2,1)} %do_hbm.1), custom_call_target="tpu_custom_call" | custom-call | tf_op jit(solution)/shard_map/pallas_call | solution.py:226
  30.6 0.0 copy-start
  30.6 2.4 %copy.13 = bf16[128,4096]{1,0:T(8,128)(2,1)} copy(bf16[128,4096]{1,0:T(8,128)(2,1)} %get-tuple-element.8) | data formatting | bytes 2097152
  33.0 0.0 copy-done
  33.0 0.0 copy-start.2
  33.0 1.0 %copy.14 = bf16[128,4096]{1,0:T(8,128)(2,1)} copy(bf16[128,4096]{1,0:T(8,128)(2,1)S(1)} %copy-done) | data formatting | bytes 2097152
  34.0 0.1 copy-done.2
  34.1 0.0 copy-start.1
  34.1 0.7 %copy.15 = bf16[128,1024]{1,0:T(8,128)(2,1)} copy(bf16[128,1024]{1,0:T(8,128)(2,1)S(1)} %copy-done.2) | data formatting | bytes 524288
  34.8 0.3 copy-done.1
  35.1 0.7 %copy.16 = bf16[128,1024]{1,0:T(8,128)(2,1)} copy(bf16[128,1024]{1,0:T(8,128)(2,1)S(1)} %copy-done.1) | data formatting | bytes 524288
Async XLA Ops:
  30.6 2.4 %copy-start = (bf16[128,4096]{1,0:T(8,128)(2,1)S(1)}, bf16[128,4096]{1,0:T(8,128)(2,1)}, u32[]{:S(2)}) copy-start(bf16[128,4096]{1,0:T(8,128)(2,1)} %get-tuple-element.9) | copy-start | bytes 3145732
  33.0 1.1 %copy-start.2 = (bf16[128,1024]{1,0:T(8,128)(2,1)S(1)}, bf16[128,1024]{1,0:T(8,128)(2,1)}, u32[]{:S(2)}) copy-start(bf16[128,1024]{1,0:T(8,128)(2,1)} %get-tuple-element.10) | copy-start | bytes 786436
  34.1 1.0 %copy-start.1 = (bf16[128,1024]{1,0:T(8,128)(2,1)S(1)}, bf16[128,1024]{1,0:T(8,128)(2,1)}, u32[]{:S(2)}) copy-start(bf16[128,1024]{1,0:T(8,128)(2,1)} %get-tuple-element.11) | copy-start | bytes 786436

commit v2 on v1

--- a/solution.py
+++ b/solution.py
@@ -14,9 +14,9 @@
 
 
 def kernel(
-    back, total, lens, q_hbm, k_hbm, v_hbm, do_hbm, att_hbm, dq_hbm, dk_hbm, dv_hbm,
-    window, qbuf, dobuf, attbuf, dqbuf, part, landed, own, summed, bias,
-    kv_in, q_in, out_sem, sum_sem, kv_send, kv_recv, g_send, g_recv,
+    back, total, lens, q_hbm, k_hbm, v_hbm, do_hbm, attbuf, dqbuf, summed,
+    window, qbuf, dobuf, part, landed, own, bias,
+    kv_in, q_in, kv_send, kv_recv, g_send, g_recv,
 ):
     rows = q_hbm.shape[0]
     kv_heads = k_hbm.shape[1] // HEAD_DIM
@@ -47,20 +47,6 @@
             (q_hbm, do_hbm)[which].at[:, columns(g, width)],
             (qbuf, dobuf)[which].at[g],
             q_in.at[which, g],
-        )
-
-    def result(g, which):
-        return pltpu.make_async_copy(
-            (attbuf, dqbuf)[which].at[g],
-            (att_hbm, dq_hbm)[which].at[:, columns(g, width)],
-            out_sem.at[which, g],
-        )
-
-    def sum_result(g, which):
-        return pltpu.make_async_copy(
-            summed.at[g, which],
-            (dk_hbm, dv_hbm)[which].at[:, columns(g, HEAD_DIM)],
-            sum_sem.at[which, g],
         )
 
     def kv_copy(g, k):
@@ -182,8 +168,6 @@
             @pl.when(me - k >= 0)
             def _():
                 g_copy(g, k).start()
-        result(g, 0).start()
-        result(g, 1).start()
 
     @pl.loop(0, kv_heads)
     def _(g):
@@ -195,8 +179,6 @@
         for k in range(1, back + 1):
             sums = sums + landed[g, k - 1].astype(jnp.float32)
         summed[g] = sums.astype(jnp.bfloat16)
-        sum_result(g, 0).start()
-        sum_result(g, 1).start()
 
     @pl.loop(0, kv_heads)
     def _(g):
@@ -208,9 +190,25 @@
             @pl.when(me - k >= 0)
             def _():
                 g_copy(g, k).wait_send()
-        for which in range(2):
-            result(g, which).wait()
-            sum_result(g, which).wait()
+
+
+def write_out(attbuf, dqbuf, summed, att_hbm, dq_hbm, dk_hbm, dv_hbm, sems):
+    kv_heads, width = attbuf.shape[0], attbuf.shape[2]
+    copies = []
+    for g in range(kv_heads):
+        wide = slice(g * width, (g + 1) * width)
+        narrow = slice(g * HEAD_DIM, (g + 1) * HEAD_DIM)
+        for which, (source, target) in enumerate((
+            (attbuf.at[g], att_hbm.at[:, wide]),
+            (dqbuf.at[g], dq_hbm.at[:, wide]),
+            (summed.at[g, 0], dk_hbm.at[:, narrow]),
+            (summed.at[g, 1], dv_hbm.at[:, narrow]),
+        )):
+            copies.append(pltpu.make_async_copy(source, target, sems.at[which, g]))
+    for copy in copies:
+        copy.start()
+    for copy in copies:
+        copy.wait()
 
 
 def solution(mesh):
@@ -223,38 +221,45 @@
         bf, f32 = jnp.bfloat16, jnp.float32
         anywhere = pl.BlockSpec(memory_space=pl.ANY)
         dma = pltpu.SemaphoreType.DMA
+        results = pl.pallas_call(
+            functools.partial(kernel, back, total),
+            out_shape=[
+                pltpu.VMEM((kv_heads, rows, width), bf),
+                pltpu.VMEM((kv_heads, rows, width), bf),
+                pltpu.VMEM((kv_heads, 2, rows, HEAD_DIM), bf),
+            ],
+            in_specs=[pl.BlockSpec(memory_space=pltpu.SMEM)] + [anywhere] * 4,
+            out_specs=[pl.BlockSpec(memory_space=pltpu.VMEM)] * 3,
+            scratch_shapes=[
+                pltpu.VMEM((kv_heads, 2, (back + 1) * rows, HEAD_DIM), bf),
+                pltpu.VMEM((kv_heads, rows, width), bf),
+                pltpu.VMEM((kv_heads, rows, width), bf),
+                pltpu.VMEM((kv_heads, 2, back * rows, HEAD_DIM), bf),
+                pltpu.VMEM((kv_heads, back, 2, rows, HEAD_DIM), bf),
+                pltpu.VMEM((kv_heads, 2, rows, HEAD_DIM), f32),
+                pltpu.VMEM(((back + 1) * rows, rows), f32),
+                dma((2, kv_heads)),
+                dma((2, kv_heads)),
+                dma((back, kv_heads)),
+                dma((back, kv_heads)),
+                dma((back, kv_heads)),
+                dma((back, kv_heads)),
+            ],
+            compiler_params=pltpu.CompilerParams(collective_id=0, has_side_effects=True),
+        )(doc_lengths, query, key, value, grad_out)
+        results = [pltpu.with_memory_space_constraint(r, pltpu.VMEM) for r in results]
         return pl.pallas_call(
-            functools.partial(kernel, back, total),
+            write_out,
             out_shape=[
                 jax.ShapeDtypeStruct(query.shape, bf),
                 jax.ShapeDtypeStruct(query.shape, bf),
                 jax.ShapeDtypeStruct(key.shape, bf),
                 jax.ShapeDtypeStruct(key.shape, bf),
             ],
-            in_specs=[pl.BlockSpec(memory_space=pltpu.SMEM)] + [anywhere] * 4,
+            in_specs=[pl.BlockSpec(memory_space=pltpu.VMEM)] * 3,
             out_specs=[anywhere] * 4,
-            scratch_shapes=[
-                pltpu.VMEM((kv_heads, 2, (back + 1) * rows, HEAD_DIM), bf),
-                pltpu.VMEM((kv_heads, rows, width), bf),
-                pltpu.VMEM((kv_heads, rows, width), bf),
-                pltpu.VMEM((kv_heads, rows, width), bf),
-                pltpu.VMEM((kv_heads, rows, width), bf),
-                pltpu.VMEM((kv_heads, 2, back * rows, HEAD_DIM), bf),
-                pltpu.VMEM((kv_heads, back, 2, rows, HEAD_DIM), bf),
-                pltpu.VMEM((kv_heads, 2, rows, HEAD_DIM), f32),
-                pltpu.VMEM((kv_heads, 2, rows, HEAD_DIM), bf),
-                pltpu.VMEM(((back + 1) * rows, rows), f32),
-                dma((2, kv_heads)),
-                dma((2, kv_heads)),
-                dma((2, kv_heads)),
-                dma((2, kv_heads)),
-                dma((back, kv_heads)),
-                dma((back, kv_heads)),
-                dma((back, kv_heads)),
-                dma((back, kv_heads)),
-            ],
-            compiler_params=pltpu.CompilerParams(collective_id=0, has_side_effects=True),
-        )(doc_lengths, query, key, value, grad_out)
+            scratch_shapes=[dma((4, kv_heads))],
+        )(*results)
 
     split = P(("blk", "head"), None)
     return jax.shard_map(

time: 36 us -> 31.6 us (0.88)
  local copies, waits for them, and re-layouts: 5.22 us -> 0 us
  Pallas kernels: 30 us -> 30.8 us
    unnamed x10 -> x0, local copies, waits for them, and re-layouts: 5.22 us -> none
    pallas_call x1 -> x2, Pallas kernels: 30 us -> 30.8 us  [the longest x1 29.1 us: per_device(): pl.pallas_call(functools.partial(kernel, back, total), out_shape=[pltpu.V...]
where the time goes in v2:
time: 31.6 us; the launch traced here: 31.5 us
  Pallas kernels  30.8 us (97%)
  between operations  0.64 us (2%)
    pallas_call x1, Pallas kernels, per_device(): pl.pallas_call(functools.partial(kernel, back, total), out_shape=[pltpu.V...  29.1 us
    pallas_call x1, Pallas kernels, per_device(): pl.pallas_call(write_out, out_shape=[jax.ShapeDtypeStruct(query.shape, bf...  1.74 us

profile of v2, /device:TPU:0, one launch (start us, length us, event | category | flops | bytes accessed | tf_op | source)
XLA Modules:
  0.0 31.5 jit_solution(15520113866229768237)
XLA Ops:
  0.6 29.1 %shard_map.84 = (bf16[8,128,512]{2,1,0:T(8,128)(2,1)S(1)}, bf16[8,128,512]{2,1,0:T(8,128)(2,1)S(1)}, bf16[8,2,128,128]{3,2,1,0:T(8,128)(2,1)S(1)}) custom-call(s32[32]{0:T(128)} %lens.1, bf16[128,4096]{1,0:T(8,128)(2,1)} %q_hbm.1, bf16[128,1024]{1,0:T(8,128)(2,1)} %k_hbm.1, bf16[128,1024]{1,0:T(8,128)(2,1)} %v_hbm.1, bf16[128,4096]{1,0:T(8,128)(2,1)} %do_hbm.1), custom_call_target="tpu_custom_call" | custom-call | tf_op jit(solution)/shard_map/pallas_call | solution.py:224
  29.7 1.7 %shard_map.85 = (bf16[128,4096]{1,0:T(8,128)(2,1)}, bf16[128,4096]{1,0:T(8,128)(2,1)}, bf16[128,1024]{1,0:T(8,128)(2,1)}, bf16[128,1024]{1,0:T(8,128)(2,1)}) custom-call(bf16[8,128,512]{2,1,0:T(8,128)(2,1)S(1)} %get-tuple-element.7.attbuf, bf16[8,128,512]{2,1,0:T(8,128)(2,1)S(1)} %get-tuple-element.8.dqbuf, bf16[8,2,128,128]{3,2,1,0:T(8,128)(2,1)S(1)} %get-tuple-element.9.summed), custom_call_target="tpu_custom_call" | custom-call | tf_op jit(solution)/shard_map/pallas_call | solution.py:251

commit v3 on v2

--- a/solution.py
+++ b/solution.py
@@ -14,7 +14,7 @@
 
 
 def kernel(
-    back, total, lens, q_hbm, k_hbm, v_hbm, do_hbm, attbuf, dqbuf, summed,
+    back, total, lens, q_hbm, k_hbm, v_hbm, do_hbm, attbuf, dqbuf, dkbuf, dvbuf,
     window, qbuf, dobuf, part, landed, own, bias,
     kv_in, q_in, kv_send, kv_recv, g_send, g_recv,
 ):
@@ -76,10 +76,6 @@
 
     barrier = pltpu.get_barrier_semaphore()
     for k in range(1, back + 1):
-        @pl.when(me + k < total)
-        def _():
-            pl.semaphore_signal(barrier, inc=1, device_id=device(me + k), device_id_type=MESH)
-
         @pl.when(me - k >= 0)
         def _():
             pl.semaphore_signal(barrier, inc=1, device_id=device(me - k), device_id_type=MESH)
@@ -89,8 +85,9 @@
         q_load(g, 0).start()
         q_load(g, 1).start()
 
-    greeted = jnp.minimum(me, back) + jnp.minimum(total - 1 - me, back)
-    pl.semaphore_wait(barrier, greeted)
+    @pl.when(me < total - 1)
+    def _():
+        pl.semaphore_wait(barrier, jnp.minimum(total - 1 - me, back))
 
     @pl.loop(0, kv_heads)
     def _(g):
@@ -162,8 +159,9 @@
         own[g, 1] = grad_value[back * rows :]
         for h in range(groups):
             at = slice(h * HEAD_DIM, (h + 1) * HEAD_DIM)
-            attbuf[g, :, at] = attended[:, at].T.astype(jnp.bfloat16)
-            dqbuf[g, :, at] = grad_query[:, at].T.astype(jnp.bfloat16)
+            to = columns(g * groups + h, HEAD_DIM)
+            attbuf[:, to] = attended[:, at].T.astype(jnp.bfloat16)
+            dqbuf[:, to] = grad_query[:, at].T.astype(jnp.bfloat16)
         for k in range(1, back + 1):
             @pl.when(me - k >= 0)
             def _():
@@ -178,7 +176,8 @@
         sums = own[g]
         for k in range(1, back + 1):
             sums = sums + landed[g, k - 1].astype(jnp.float32)
-        summed[g] = sums.astype(jnp.bfloat16)
+        dkbuf[:, columns(g, HEAD_DIM)] = sums[0].astype(jnp.bfloat16)
+        dvbuf[:, columns(g, HEAD_DIM)] = sums[1].astype(jnp.bfloat16)
 
     @pl.loop(0, kv_heads)
     def _(g):
@@ -192,19 +191,16 @@
                 g_copy(g, k).wait_send()
 
 
-def write_out(attbuf, dqbuf, summed, att_hbm, dq_hbm, dk_hbm, dv_hbm, sems):
-    kv_heads, width = attbuf.shape[0], attbuf.shape[2]
+def write_out(att, dq, dk, dv, att_hbm, dq_hbm, dk_hbm, dv_hbm, sems):
     copies = []
-    for g in range(kv_heads):
-        wide = slice(g * width, (g + 1) * width)
-        narrow = slice(g * HEAD_DIM, (g + 1) * HEAD_DIM)
-        for which, (source, target) in enumerate((
-            (attbuf.at[g], att_hbm.at[:, wide]),
-            (dqbuf.at[g], dq_hbm.at[:, wide]),
-            (summed.at[g, 0], dk_hbm.at[:, narrow]),
-            (summed.at[g, 1], dv_hbm.at[:, narrow]),
-        )):
-            copies.append(pltpu.make_async_copy(source, target, sems.at[which, g]))
+    pairs = ((att, att_hbm), (dq, dq_hbm), (dk, dk_hbm), (dv, dv_hbm))
+    for which, (source, target) in enumerate(pairs):
+        step = source.shape[0] // sems.shape[1]
+        for piece in range(sems.shape[1]):
+            at = slice(piece * step, (piece + 1) * step)
+            copies.append(
+                pltpu.make_async_copy(source.at[at], target.at[at], sems.at[which, piece])
+            )
     for copy in copies:
         copy.start()
     for copy in copies:
@@ -224,12 +220,13 @@
         results = pl.pallas_call(
             functools.partial(kernel, back, total),
             out_shape=[
-                pltpu.VMEM((kv_heads, rows, width), bf),
-                pltpu.VMEM((kv_heads, rows, width), bf),
-                pltpu.VMEM((kv_heads, 2, rows, HEAD_DIM), bf),
+                pltpu.VMEM(query.shape, bf),
+                pltpu.VMEM(query.shape, bf),
+                pltpu.VMEM(key.shape, bf),
+                pltpu.VMEM(key.shape, bf),
             ],
             in_specs=[pl.BlockSpec(memory_space=pltpu.SMEM)] + [anywhere] * 4,
-            out_specs=[pl.BlockSpec(memory_space=pltpu.VMEM)] * 3,
+            out_specs=[pl.BlockSpec(memory_space=pltpu.VMEM)] * 4,
             scratch_shapes=[
                 pltpu.VMEM((kv_heads, 2, (back + 1) * rows, HEAD_DIM), bf),
                 pltpu.VMEM((kv_heads, rows, width), bf),
@@ -256,9 +253,9 @@
                 jax.ShapeDtypeStruct(key.shape, bf),
                 jax.ShapeDtypeStruct(key.shape, bf),
             ],
-            in_specs=[pl.BlockSpec(memory_space=pltpu.VMEM)] * 3,
+            in_specs=[pl.BlockSpec(memory_space=pltpu.VMEM)] * 4,
             out_specs=[anywhere] * 4,
-            scratch_shapes=[dma((4, kv_heads))],
+            scratch_shapes=[dma((4, 4))],
         )(*results)
 
     split = P(("blk", "head"), None)

time: 31.6 us -> 31.5 us (level)
  no operation moved by 1% of the time
where the time goes in v3:
time: 31.5 us; the launch traced here: 31.4 us
  Pallas kernels  30.7 us (97%)
  between operations  0.64 us (2%)
    pallas_call x1, Pallas kernels, per_device(): pl.pallas_call(functools.partial(kernel, back, total), out_shape=[pltpu.V...  29.1 us
    pallas_call x1, Pallas kernels, per_device(): pl.pallas_call(write_out, out_shape=[jax.ShapeDtypeStruct(query.shape, bf...  1.61 us

profile of v3, /device:TPU:0, one launch (start us, length us, event | category | flops | bytes accessed | tf_op | source)
XLA Modules:
  0.0 31.4 jit_solution(12154878510168784728)
XLA Ops:
  0.6 29.1 %shard_map.84 = (bf16[128,4096]{1,0:T(8,128)(2,1)S(1)}, bf16[128,4096]{1,0:T(8,128)(2,1)S(1)}, bf16[128,1024]{1,0:T(8,128)(2,1)S(1)}, bf16[128,1024]{1,0:T(8,128)(2,1)S(1)}) custom-call(s32[32]{0:T(128)} %lens.1, bf16[128,4096]{1,0:T(8,128)(2,1)} %q_hbm.1, bf16[128,1024]{1,0:T(8,128)(2,1)} %k_hbm.1, bf16[128,1024]{1,0:T(8,128)(2,1)} %v_hbm.1, ...), custom_call_target="tpu_custom_call" | custom-call | tf_op jit(solution)/shard_map/pallas_call | solution.py:220
  29.8 1.6 %shard_map.85 = (bf16[128,4096]{1,0:T(8,128)(2,1)}, bf16[128,4096]{1,0:T(8,128)(2,1)}, bf16[128,1024]{1,0:T(8,128)(2,1)}, bf16[128,1024]{1,0:T(8,128)(2,1)}) custom-call(bf16[128,4096]{1,0:T(8,128)(2,1)S(1)} %get-tuple-element.8.att, bf16[128,4096]{1,0:T(8,128)(2,1)S(1)} %get-tuple-element.9.dq, bf16[128,1024]{1,0:T(8,128)(2,1)S(1)} %get-tuple-element.10.dk, ...), custom_call_target="tpu_custom_call" | custom-call | tf_op jit(solution)/shard_map/pallas_call | solution.py:248

commit v4 on v3

--- a/solution.py
+++ b/solution.py
@@ -80,11 +80,6 @@
         def _():
             pl.semaphore_signal(barrier, inc=1, device_id=device(me - k), device_id_type=MESH)
 
-    @pl.loop(0, kv_heads)
-    def _(g):
-        q_load(g, 0).start()
-        q_load(g, 1).start()
-
     @pl.when(me < total - 1)
     def _():
         pl.semaphore_wait(barrier, jnp.minimum(total - 1 - me, back))
@@ -97,6 +92,11 @@
             @pl.when(me + k < total)
             def _():
                 kv_copy(g, k).start()
+
+    @pl.loop(0, kv_heads)
+    def _(g):
+        q_load(g, 0).start()
+        q_load(g, 1).start()
 
     for k in range(1, back + 1):
         @pl.when(me - k < 0)

time: 31.5 us -> 31.6 us (level)
  no operation moved by 1% of the time
where the time goes in v4:
time: 31.6 us; the launch traced here: 31.4 us
  Pallas kernels  30.7 us (97%)
  between operations  0.64 us (2%)
    pallas_call x1, Pallas kernels, per_device(): pl.pallas_call(functools.partial(kernel, back, total), out_shape=[pltpu.V...  29.1 us
    pallas_call x1, Pallas kernels, per_device(): pl.pallas_call(write_out, out_shape=[jax.ShapeDtypeStruct(query.shape, bf...  1.61 us

profile of v4, /device:TPU:0, one launch (start us, length us, event | category | flops | bytes accessed | tf_op | source)
XLA Modules:
  0.0 31.4 jit_solution(2896952167562595620)
XLA Ops:
  0.6 29.1 %shard_map.84 = (bf16[128,4096]{1,0:T(8,128)(2,1)S(1)}, bf16[128,4096]{1,0:T(8,128)(2,1)S(1)}, bf16[128,1024]{1,0:T(8,128)(2,1)S(1)}, bf16[128,1024]{1,0:T(8,128)(2,1)S(1)}) custom-call(s32[32]{0:T(128)} %lens.1, bf16[128,4096]{1,0:T(8,128)(2,1)} %q_hbm.1, bf16[128,1024]{1,0:T(8,128)(2,1)} %k_hbm.1, bf16[128,1024]{1,0:T(8,128)(2,1)} %v_hbm.1, ...), custom_call_target="tpu_custom_call" | custom-call | tf_op jit(solution)/shard_map/pallas_call | solution.py:220
  29.8 1.6 %shard_map.85 = (bf16[128,4096]{1,0:T(8,128)(2,1)}, bf16[128,4096]{1,0:T(8,128)(2,1)}, bf16[128,1024]{1,0:T(8,128)(2,1)}, bf16[128,1024]{1,0:T(8,128)(2,1)}) custom-call(bf16[128,4096]{1,0:T(8,128)(2,1)S(1)} %get-tuple-element.8.att, bf16[128,4096]{1,0:T(8,128)(2,1)S(1)} %get-tuple-element.9.dq, bf16[128,1024]{1,0:T(8,128)(2,1)S(1)} %get-tuple-element.10.dk, ...), custom_call_target="tpu_custom_call" | custom-call | tf_op jit(solution)/shard_map/pallas_call | solution.py:248
